TPU v7x, 32 devices: a 4x4x1 block of a 4x4x8 slice. The times are simulated.
32 devices in a mesh: replica: 1 (over z), tp: 4 (over y), stage: 8 (over x, core).
Axes of the slice: x: 4, y: 4, z: 1, core: 2. Of those that a mesh axis runs over, the one named last changes fastest.
The devices are a block of a 4x4x8 slice.
Arguments:
- embeds: bfloat16 [32, 2, 2048], P('replica')
- w_qkv: bfloat16 [8, 2048, 8, 4, 128], P('stage', None, 'tp')
- w_out: bfloat16 [8, 2048, 2048], P('stage', 'tp')
- w_gate: bfloat16 [8, 2048, 6144], P('stage', None, 'tp')
- w_up: bfloat16 [8, 2048, 6144], P('stage', None, 'tp')
- w_down: bfloat16 [8, 6144, 2048], P('stage', 'tp')
- norm_gain: float32 [8, 2, 2048], P('stage')
- k_cache: bfloat16 [8, 32, 2, 16, 8, 128], P('stage', 'replica', None, None, 'tp')
- v_cache: bfloat16 [8, 32, 2, 16, 8, 128], P('stage', 'replica', None, None, 'tp')
- lengths: int32 [32, 2], P('replica')
- final_gain: float32 [2048], replicated
- w_unembed: bfloat16 [2048, 151936], P(None, ('stage', 'tp'))
Outputs:
- output 1: float32 [32, 2, 151936], P('replica', None, ('stage', 'tp'))
- output 2: bfloat16 [8, 32, 2, 16, 8, 128], P('stage', 'replica', None, None, 'tp')
- output 3: bfloat16 [8, 32, 2, 16, 8, 128], P('stage', 'replica', None, None, 'tp')
All inputs are finite; a program needn't handle non-finite values.
Results may differ from a plain program's by a relative error of at most 0.02.
Values are sent between devices in bfloat16 or wider.
A program may use at most 768 MiB of HBM per device.

v0:
```python
import jax
import jax.numpy as jnp
from jax import lax
from jax.sharding import PartitionSpec as P

NORM_EPS = 1e-5
ROPE_THETA = 10000.0


def rms_norm(values, gain_row):
    mean_sq = jnp.mean(values * values, axis=-1, keepdims=True)
    return (values * lax.rsqrt(mean_sq + NORM_EPS) * gain_row).astype(jnp.bfloat16)


def rotate_half(values, cos_part, sin_part):
    half_dim = values.shape[-1] // 2
    first_half = values[..., :half_dim]
    second_half = values[..., half_dim:]
    return jnp.concatenate([first_half * cos_part - second_half * sin_part, second_half * cos_part + first_half * sin_part], axis=-1)


def rope_tables(lengths, head_dim):
    inv_freq = ROPE_THETA ** (-jnp.arange(head_dim // 2, dtype=jnp.float32) * (2.0 / head_dim))
    angles = lengths.astype(jnp.float32)[..., None] * inv_freq
    return jnp.cos(angles), jnp.sin(angles)


def store_group(store_buf, new_rows, group_slot, is_valid, axis_pos):
    kept_rows = lax.dynamic_index_in_dim(store_buf, group_slot, axis_pos, keepdims=False)
    return lax.dynamic_update_index_in_dim(store_buf, jnp.where(is_valid, new_rows, kept_rows), group_slot, axis_pos)


def stage_layers(residual, lengths_row, w_qkv, w_out, w_gate, w_up, w_down, norm_gain, k_group, v_group):
    batch_rows, width = residual.shape
    layer_count = w_qkv.shape[0]
    kv_local = w_qkv.shape[2]
    slot_count = w_qkv.shape[3]
    head_dim = w_qkv.shape[4]
    q_per_kv = slot_count - 2
    cos_part, sin_part = rope_tables(lengths_row, head_dim)
    cos_q = cos_part[:, None, None, :]
    sin_q = sin_part[:, None, None, :]
    cos_k = cos_part[:, None, :]
    sin_k = sin_part[:, None, :]
    visible = (jnp.arange(k_group.shape[2])[None, :] < lengths_row[:, None])[:, None, None, :]
    score_scale = head_dim ** -0.5
    key_rows = []
    val_rows = []
    for layer_idx in range(layer_count):
        normed = rms_norm(residual, norm_gain[layer_idx, 0])
        proj_out = jnp.dot(normed, w_qkv[layer_idx].reshape(width, kv_local * slot_count * head_dim), preferred_element_type=jnp.float32).reshape(batch_rows, kv_local, slot_count, head_dim)
        queries = rotate_half(proj_out[:, :, :q_per_kv], cos_q, sin_q).astype(jnp.bfloat16)
        key_new = rotate_half(proj_out[:, :, q_per_kv], cos_k, sin_k).astype(jnp.bfloat16)
        val_new = proj_out[:, :, q_per_kv + 1].astype(jnp.bfloat16)
        old_scores = jnp.einsum('bkqn,btkn->bkqt', queries, k_group[layer_idx], preferred_element_type=jnp.float32) * score_scale
        old_scores = jnp.where(visible, old_scores, -jnp.inf)
        new_score = jnp.einsum('bkqn,bkn->bkq', queries, key_new, preferred_element_type=jnp.float32) * score_scale
        peak_score = jnp.maximum(jnp.max(old_scores, axis=-1), new_score)
        old_exp = jnp.exp(old_scores - peak_score[..., None])
        new_exp = jnp.exp(new_score - peak_score)
        denom_sum = jnp.sum(old_exp, axis=-1) + new_exp
        old_probs = (old_exp / denom_sum[..., None]).astype(jnp.bfloat16)
        new_probs = (new_exp / denom_sum).astype(jnp.bfloat16)
        attn_out = jnp.einsum('bkqt,btkn->bkqn', old_probs, v_group[layer_idx], preferred_element_type=jnp.float32)
        attn_out = attn_out + jnp.einsum('bkq,bkn->bkqn', new_probs, val_new, preferred_element_type=jnp.float32)
        attn_flat = attn_out.astype(jnp.bfloat16).reshape(batch_rows, kv_local * q_per_kv * head_dim)
        residual = residual + lax.psum(jnp.dot(attn_flat, w_out[layer_idx], preferred_element_type=jnp.float32), 'tp')
        normed_mlp = rms_norm(residual, norm_gain[layer_idx, 1])
        gate_act = jnp.dot(normed_mlp, w_gate[layer_idx], preferred_element_type=jnp.float32)
        up_act = jnp.dot(normed_mlp, w_up[layer_idx], preferred_element_type=jnp.float32)
        hidden = (jax.nn.silu(gate_act) * up_act).astype(jnp.bfloat16)
        residual = residual + lax.psum(jnp.dot(hidden, w_down[layer_idx], preferred_element_type=jnp.float32), 'tp')
        key_rows.append(key_new)
        val_rows.append(val_new)
    return residual, jnp.stack(key_rows), jnp.stack(val_rows)


def solution(mesh):
    stages = mesh.shape['stage']
    cache_spec = P('stage', 'replica', None, None, 'tp', None)
    in_specs = (P('replica'), P('stage', None, 'tp', None, None), P('stage', 'tp', None), P('stage', None, 'tp'), P('stage', None, 'tp'), P('stage', 'tp', None), P('stage'), cache_spec, cache_spec, P('replica'), P(), P(None, ('stage', 'tp')))
    out_specs = (P('replica', None, ('stage', 'tp')), cache_spec, cache_spec)
    next_stage = [(src_idx, src_idx + 1) for src_idx in range(stages - 1)]

    def device_step(embeds, w_qkv, w_out, w_gate, w_up, w_down, norm_gain, k_cache, v_cache, lengths, final_gain, w_unembed):
        group_count, batch_rows, width = embeds.shape
        stage_idx = lax.axis_index('stage')
        row_shape = (k_cache.shape[0], group_count, batch_rows, k_cache.shape[4], k_cache.shape[5])

        def tick_body(tick_idx, loop_state):
            incoming, key_store, val_store, final_rows = loop_state
            group_idx = tick_idx - stage_idx
            is_valid = jnp.logical_and(group_idx >= 0, group_idx < group_count)
            group_slot = jnp.clip(group_idx, 0, group_count - 1)
            first_in = lax.dynamic_index_in_dim(embeds, group_slot, 0, keepdims=False)
            residual = jnp.where(stage_idx == 0, first_in, incoming).astype(jnp.float32)
            lengths_row = lax.dynamic_index_in_dim(lengths, group_slot, 0, keepdims=False)
            k_group = lax.dynamic_index_in_dim(k_cache, group_slot, 1, keepdims=False)
            v_group = lax.dynamic_index_in_dim(v_cache, group_slot, 1, keepdims=False)
            residual, key_rows, val_rows = stage_layers(residual, lengths_row, w_qkv, w_out, w_gate, w_up, w_down, norm_gain, k_group, v_group)
            hidden_out = residual.astype(jnp.bfloat16)
            key_store = store_group(key_store, key_rows, group_slot, is_valid, 1)
            val_store = store_group(val_store, val_rows, group_slot, is_valid, 1)
            final_rows = store_group(final_rows, hidden_out, group_slot, is_valid, 0)
            incoming = lax.ppermute(hidden_out, 'stage', next_stage)
            return incoming, key_store, val_store, final_rows

        start_state = (jnp.zeros((batch_rows, width), jnp.bfloat16), jnp.zeros(row_shape, jnp.bfloat16), jnp.zeros(row_shape, jnp.bfloat16), jnp.zeros((group_count, batch_rows, width), jnp.bfloat16))
        loop_out = lax.fori_loop(0, group_count + stages - 1, tick_body, start_state)
        final_all = lax.psum(jnp.where(stage_idx == stages - 1, loop_out[3], jnp.zeros_like(loop_out[3])), 'stage')
        normed_out = rms_norm(final_all.astype(jnp.float32), final_gain).reshape(group_count * batch_rows, width)
        logits = jnp.dot(normed_out, w_unembed, preferred_element_type=jnp.float32).reshape(group_count, batch_rows, w_unembed.shape[1])
        write_mask = (jnp.arange(k_cache.shape[3])[None, None, :] == lengths[:, :, None])[None, :, :, :, None, None]
        k_out = jnp.where(write_mask, loop_out[1][:, :, :, None], k_cache)
        v_out = jnp.where(write_mask, loop_out[2][:, :, :, None], v_cache)
        return logits, k_out, v_out

    return jax.shard_map(device_step, mesh=mesh, in_specs=in_specs, out_specs=out_specs, check_vma=False)
```

profile of v0, /device:TPU:97, one launch (start us, length us, event | category | flops | bytes accessed | tf_op | source)
XLA Modules:
  0.0 2114.9 jit_solution(1966233961241718154)
XLA Ops:
  17.2 2021.7 %while.20 = (s32[]{:T(128)}, bf16[2,2048]{1,0:T(2,128)(2,1)S(1)}, bf16[1,32,2,2,128]{4,2,3,1,0:T(2,128)(2,1)S(1)}, bf16[1,32,2,2,128]{4,2,3,1,0:T(2,128)(2,1)}, ...) while((s32[]{:T(128)}, bf16[2,2048]{1,0:T(2,128)(2,1)S(1)}, ...), condition=%wide.region_7.8_spmd, body=%wide.region_0.7_spmd.sunk | while | flops 50556772 | bytes 25728968 | solution.py:109
  23.9 15.9 psum.34
  79.8 11.7 psum.34
  131.6 11.7 psum.34
  183.3 11.7 psum.34
  235.0 11.7 psum.34
  286.8 11.7 psum.34
  338.5 11.7 psum.34
  390.2 11.6 psum.34
  441.9 11.6 psum.34
  493.7 11.6 psum.34
  545.4 11.6 psum.34
  597.1 11.6 psum.34
  648.8 11.6 psum.34
  700.6 11.6 psum.34
  752.3 11.6 psum.34
  804.0 11.6 psum.34
  855.7 11.6 psum.34
  907.5 11.6 psum.34
  959.2 11.6 psum.34
  1010.9 11.6 psum.34
  1062.7 11.6 psum.34
  2044.0 48.4 %all-reduce.2.cloned.1.call-done = bf16[32,2,2048]{2,0,1:T(8,128)(2,1)} async-done(((bf16[32,2,2048]{2,0,1:T(8,128)(2,1)}), bf16[32,2,2048]{2,0,1:T(8,128)(2,1)}) %all-reduce.2.cloned.1.call-update) | async-done | bytes 262160 | tf_op jit(solution)/shard_map/psum | solution.py:110
  2093.4 12.7 fusion.42
  (1370 shorter events, 1787.9 us)
Async XLA Ops:
  7.2 2085.1 %all-reduce.2.cloned.1.call-start = ((), (), s32[]{:S(2)}) async-start(), calls=%async_computation | async-start | bytes 524288 | tf_op jit(solution)/shard_map/psum | solution.py:110
  888.6 12.3 collective-permute-start
  940.3 12.3 collective-permute-start
  992.0 12.3 collective-permute-start
  1043.7 12.3 collective-permute-start
  1095.4 12.3 collective-permute-start
  1147.2 12.3 collective-permute-start
  1198.9 12.3 collective-permute-start
  1250.6 12.4 collective-permute-start
  1302.3 12.4 collective-permute-start
  1354.1 12.4 collective-permute-start
  1405.8 12.4 collective-permute-start
  1457.5 12.4 collective-permute-start
  1509.2 12.4 collective-permute-start
  1561.0 12.4 collective-permute-start
  1612.7 12.4 collective-permute-start
  1664.4 12.4 collective-permute-start
  1716.1 12.4 collective-permute-start
  1767.9 12.4 collective-permute-start
  1819.6 12.4 collective-permute-start
  1871.3 12.4 collective-permute-start
  1923.0 12.4 collective-permute-start
  1974.7 12.4 collective-permute-start
  2026.5 12.4 collective-permute-start
  (21 other events, 2312.1 us)
Sparse Core Ops, SparseCore 0:
  2039.9 52.3 all-reduce.1
where the time goes:
time: 2130 us; the launch traced here: 2110 us
  blocking collectives  880 us (41%)
  matrix products  574 us (27%)
  starting transfers between devices  431 us (20%)
  other arithmetic  149 us (7%)
  waiting for transfers between devices  48.5 us (2%)
    psum x39, blocking collectives, stage_layers(): lax.psum(jnp.dot(attn_flat, w_out[layer_idx], preferred_element_type=jnp....  457 us
    ppermute x39, starting transfers between devices, tick_body(): incoming = lax.ppermute(hidden_out, 'stage', next_stage)  431 us
    psum x39, blocking collectives, stage_layers(): lax.psum(jnp.dot(hidden, w_down[layer_idx], preferred_element_type=jnp.fl...  423 us
    dot_general x39, matrix products, stage_layers(): jnp.dot(hidden, w_down[layer_idx], preferred_element_type=jnp.float32)  249 us
    dot_general x39, matrix products, stage_layers(): jnp.dot(normed_mlp, w_gate[layer_idx], preferred_element_type=jnp.float32)  146 us
    dot_general x39, matrix products, stage_layers(): jnp.dot(normed, w_qkv[layer_idx].reshape(width, kv_local * slot_count * h...  131 us
    dynamic_update_slice x78, other arithmetic, store_group(): lax.dynamic_update_index_in_dim(store_buf, jnp.where(is_valid, new_rows,...  50.3 us
    psum x1, waiting for transfers between devices, device_step(): lax.psum(jnp.where(stage_idx == stages - 1, loop_out[3], jnp.zeros_like(l...  48.4 us
  transfers between devices with their start and end apart: 40, of which 1 were waited for; matrix products, arithmetic and copies ran while one was open for 3% of the time, Pallas kernels for 0%

commit v1 on v0

v1 whole, which is shorter than its diff:
```python
import functools

import numpy as np
import jax
import jax.numpy as jnp
from jax import lax
from jax.experimental import pallas as pl
from jax.experimental.pallas import tpu as pltpu
from jax.sharding import PartitionSpec as P

NORM_EPS = 1e-5
ROPE_THETA = 10000.0
ROWS = 8
F32 = jnp.float32
BF16 = jnp.bfloat16
MESH = pl.DeviceIdType.MESH


def rope_rows(positions, head_dim):
    half = head_dim // 2
    inv_freq = (np.float32(ROPE_THETA) ** (-np.arange(half, dtype=np.float32) * np.float32(2.0 / head_dim))).astype(np.float32)
    angles = np.arange(positions, dtype=np.float32)[:, None] * inv_freq[None, :]
    cos, sin = np.cos(angles), np.sin(angles)
    return np.stack([np.concatenate([cos, cos], -1), np.concatenate([-sin, sin], -1)]).astype(np.float32)


def normed(values, gain):
    mean_sq = jnp.mean(values * values, axis=-1, keepdims=True)
    return (values * lax.rsqrt(mean_sq + NORM_EPS) * gain).astype(BF16)


def step_kernel(dims, emb, wq_raw, wo_h, wg_h, wu_h, wd_h, gains_h, kc_h, vc_h, lens, rope_h, fgain_h, wv_h,
                logits_h, ko_h, vo_h,
                raw, stage32, wq, wo, wg, wu, wd, gains, kc, vc, rope, fgain, wv, rin, res, hid, ar1, part, rs2, outs, fin, cosb, sinb, xn, logits,
                ld, ldq, lo, ar1_s, ar1_r, rs2_s, rs2_r, ag_s, ag_r, fin_s, fin_r):
    tp, stages, chunks, kvs, slots, hd, ctx = dims
    qpk = slots - 2
    nh = kvs * qpk
    width = wo.shape[1]
    cw = width // tp
    ff = wg.shape[1]
    me = lax.axis_index("tp")
    st = lax.axis_index("stage")
    total = tp * stages
    mine = st * tp + me
    last = stages - 1
    krows = ROWS * ctx * kvs

    def dev(flat):
        return {"stage": flat // tp, "tp": lax.rem(flat, tp)}

    cpl = lambda s, d, k: pltpu.make_async_copy(s, d, ld.at[k])
    qrows = raw.shape[0] // 8
    qc = [pltpu.make_async_copy(wq_raw.at[pl.ds(i * qrows, qrows)], raw.at[pl.ds(i * qrows, qrows)], ldq.at[i]) for i in range(8)]
    loads = [cpl(gains_h, gains, 0), cpl(rope_h, rope, 1), cpl(kc_h, kc, 2), cpl(vc_h, vc, 3), cpl(wo_h, wo, 4), cpl(wg_h, wg, 5), cpl(wu_h, wu, 6), cpl(wd_h, wd, 7), cpl(fgain_h, fgain, 8), cpl(wv_h, wv, 9)]
    emb_load = cpl(emb, rin, 10)

    for c in qc[:2]:
        c.start()

    @pl.when(st == 0)
    def _():
        emb_load.start()

    for c in loads[:2]:
        c.start()
    for c in qc[2:]:
        c.start()
    for c in loads[2:]:
        c.start()

    barrier = pltpu.get_barrier_semaphore()

    def greet(k, _):
        pl.semaphore_signal(barrier, inc=1, device_id=dev(lax.rem(mine + k, total)), device_id_type=MESH)
        return 0

    lax.fori_loop(1, total, greet, 0)

    row8 = lax.broadcasted_iota(jnp.int32, (ROWS, hd), 0)

    def lens_of(c):
        return [lens[i % 2, c * (ROWS // 2) + i // 2] for i in range(ROWS)]

    loads[1].wait()

    def rope_body(c, _):
        len8 = jnp.zeros((ROWS, hd), jnp.int32)
        for i, v in enumerate(lens_of(c)):
            len8 = jnp.where(row8 == i, v, len8)
        cs = jnp.zeros((ROWS, hd), F32)
        sn = jnp.zeros((ROWS, hd), F32)
        for p in range(ctx):
            cs = jnp.where(len8 == p, rope[0, p:p + 1, :], cs)
            sn = jnp.where(len8 == p, rope[1, p:p + 1, :], sn)
        cosb[c] = cs
        sinb[c] = sn
        return 0

    lax.fori_loop(0, chunks, rope_body, 0)

    nslot = kvs * slots
    kq = qrows // nslot
    for i in range(8):
        qc[i].wait()
        stage32[...] = raw[pl.ds(i * qrows, qrows), :].astype(F32)
        for s in range(nslot):
            wq[pl.ds(i * kq, kq), pl.ds(s * hd, hd)] = stage32[pl.ds(s, kq, stride=nslot), :].astype(BF16)

    loads[0].wait()

    @pl.when(st == 0)
    def _():
        emb_load.wait()

    pl.semaphore_wait(barrier, total - 1)

    scale = hd ** -0.5

    def ar1_copy(c, slot, d, peer):
        return pltpu.make_async_remote_copy(src_ref=ar1.at[c, slot], dst_ref=ar1.at[c, slot], send_sem=ar1_s.at[c, d], recv_sem=ar1_r.at[c, slot], device_id={"tp": peer}, device_id_type=MESH)

    def rs2_copy(c, slot, d, peer):
        return pltpu.make_async_remote_copy(src_ref=part.at[c, peer], dst_ref=rs2.at[c, slot], send_sem=rs2_s.at[c, d], recv_sem=rs2_r.at[c, slot], device_id={"tp": peer}, device_id_type=MESH)

    def ag_copy(c, slot, d, peer, nxt):
        return pltpu.make_async_remote_copy(src_ref=outs.at[c], dst_ref=rin.at[c, slot], send_sem=ag_s.at[c, d], recv_sem=ag_r.at[c, slot], device_id={"stage": nxt, "tp": peer}, device_id_type=MESH)

    def fin_copy(c, slot, flat):
        return pltpu.make_async_remote_copy(src_ref=outs.at[c], dst_ref=fin.at[c * tp + slot], send_sem=fin_s.at[c], recv_sem=fin_r.at[c, slot], device_id=dev(flat), device_id_type=MESH)

    def attn_part(c):
        @pl.when(st > 0)
        def _():
            for s in range(tp):
                ag_copy(c, s, s, s, 0).wait_recv()

        x = jnp.concatenate([rin[c, s] for s in range(tp)], axis=1).astype(F32)
        u = normed(x, gains[0:1, :])
        proj = jnp.dot(u, wq[...], preferred_element_type=F32)
        cs, sn = cosb[c], sinb[c]

        def rot(v):
            return v * cs + pltpu.roll(v, hd // 2, 1) * sn

        qs, kn, vn = [], [], []
        for kv in range(kvs):
            for j in range(slots):
                o = (kv * slots + j) * hd
                v = proj[:, o:o + hd]
                if j < qpk:
                    qs.append(rot(v))
                elif j == qpk:
                    kn.append(rot(v).astype(BF16).astype(F32))
                else:
                    vn.append(v.astype(BF16).astype(F32))
        qb = jnp.concatenate(qs, axis=0).astype(BF16)
        k_rep = jnp.concatenate([kn[h // qpk] for h in range(nh)], axis=0)
        v_rep = jnp.concatenate([vn[h // qpk] for h in range(nh)], axis=0)

        @pl.when(c == 0)
        def _():
            loads[2].wait()
            loads[3].wait()

        ks = pl.ds(pl.multiple_of(c * krows, krows), krows)
        s_old = lax.dot_general(qb, kc[ks, :], (((1,), (1,)), ((), ())), preferred_element_type=F32) * scale
        s_new = jnp.sum(qb.astype(F32) * k_rep, axis=-1, keepdims=True) * scale
        lvals = lens_of(c)
        rr = lax.broadcasted_iota(jnp.int32, (nh * ROWS, krows), 0)
        cc = lax.broadcasted_iota(jnp.int32, (nh * ROWS, krows), 1)
        rs = lax.rem(rr, ROWS)
        lrow = jnp.zeros((nh * ROWS, krows), jnp.int32)
        for i, v in enumerate(lvals):
            lrow = jnp.where(rs == i, v, lrow)
        visible = (rs == cc // (ctx * kvs)) & (rr // (qpk * ROWS) == lax.rem(cc, kvs)) & (lax.rem(cc // kvs, ctx) < lrow)
        s_old = jnp.where(visible, s_old, -1e30)
        peak = jnp.maximum(jnp.max(s_old, axis=-1, keepdims=True), s_new)
        p_old = jnp.where(visible, jnp.exp(s_old - peak), 0.0)
        p_new = jnp.exp(s_new - peak)
        den = jnp.sum(p_old, axis=-1, keepdims=True) + p_new
        pb = (p_old / den).astype(BF16)
        pn = (p_new / den).astype(BF16).astype(F32)
        at = jnp.dot(pb, vc[ks, :], preferred_element_type=F32) + pn * v_rep
        flat = jnp.concatenate([at[h * ROWS:(h + 1) * ROWS, :] for h in range(nh)], axis=1).astype(BF16)

        @pl.when(c == 0)
        def _():
            loads[4].wait()

        ar1[c, me] = jnp.dot(flat, wo[...], preferred_element_type=F32)
        for d in (2, 1, 3):
            ar1_copy(c, me, d, lax.rem(me + d, tp)).start()

        half = lax.broadcasted_iota(jnp.int32, (ctx * kvs, hd), 0)
        sel = lax.rem(half, kvs)
        pos = half // kvs
        for buf, new, out_h, sem in ((kc, kn, ko_h, 0), (vc, vn, vo_h, 1)):
            for i in range(ROWS):
                rows = pl.ds(pl.multiple_of(c * krows + i * ctx * kvs, ctx * kvs), ctx * kvs)
                cand = jnp.broadcast_to(new[0][i:i + 1, :], (ctx * kvs, hd))
                for h in range(1, kvs):
                    cand = jnp.where(sel == h, new[h][i:i + 1, :], cand)
                buf[rows, :] = jnp.where(pos == lvals[i], cand, buf[rows, :].astype(F32)).astype(BF16)
            pltpu.make_async_copy(buf.at[ks], out_h.at[ks], lo.at[sem, c]).start()

    def mlp_up(c):
        for d in range(1, tp):
            s = lax.rem(me + d, tp)
            ar1_copy(c, s, d, s).wait_recv()
        x = jnp.concatenate([rin[c, s] for s in range(tp)], axis=1).astype(F32)
        tot = ar1[c, 0]
        for s in range(1, tp):
            tot = tot + ar1[c, s]
        r = x + tot
        for s in range(tp):
            res[c, s] = r[:, s * cw:(s + 1) * cw]
        u = normed(r, gains[1:2, :])

        @pl.when(c == 0)
        def _():
            loads[5].wait()
            loads[6].wait()

        g = jnp.dot(u, wg[...], preferred_element_type=F32)
        up = jnp.dot(u, wu[...], preferred_element_type=F32)
        hid[...] = (g * jax.nn.sigmoid(g)) * up

    def mlp_down(c):
        @pl.when(c == 0)
        def _():
            loads[7].wait()

        y = jnp.dot(hid[...].astype(BF16), wd[...], preferred_element_type=F32)
        for s in range(tp):
            part[c, s] = y[:, s * cw:(s + 1) * cw]
        for d in (2, 1, 3):
            rs2_copy(c, me, d, lax.rem(me + d, tp)).start()
        rs2[c, me] = part[c, me]

    def stage_end(c):
        for d in range(1, tp):
            s = lax.rem(me + d, tp)
            rs2_copy(c, s, d, s).wait_recv()
        tot = rs2[c, 0]
        for s in range(1, tp):
            tot = tot + rs2[c, s]
        outs[c] = (res[c, me] + tot).astype(BF16)

        @pl.when(st < last)
        def _():
            for d in (2, 1, 3, 0):
                ag_copy(c, me, d, lax.rem(me + d, tp), st + 1).start()

        @pl.when(st == last)
        def _():
            def send(k, _):
                fin_copy(c, me, lax.rem(mine + k, total)).start()
                return 0

            lax.fori_loop(1, total, send, 0)
            fin[c * tp + me] = outs[c]

    def tick(i, _):
        @pl.when(i < chunks)
        def _():
            attn_part(i)

        @pl.when((i >= 1) & (i <= chunks))
        def _():
            mlp_up(i - 1)

        @pl.when(i >= 2)
        def _():
            stage_end(i - 2)

        @pl.when((i >= 1) & (i <= chunks))
        def _():
            mlp_down(i - 1)

        return 0

    lax.fori_loop(0, chunks + 2, tick, 0)

    loads[8].wait()
    for c in range(chunks):
        for s in range(tp):
            @pl.when((st < last) | (me != s))
            def _():
                fin_copy(c, s, s).wait_recv()
    for p in range(chunks // 2):
        rows = [jnp.concatenate([fin[c * tp + s] for s in range(tp)], axis=1).astype(F32) for c in (2 * p, 2 * p + 1)]
        xn[2 * p * ROWS:(2 * p + 2) * ROWS, :] = normed(jnp.concatenate(rows, axis=0), fgain[...])
    loads[9].wait()
    vocab = wv.shape[0]
    tile = 768
    full = vocab // tile

    def vocab_tile(j, _):
        o = pl.multiple_of(j * tile, tile)
        logits[:, pl.ds(o, tile)] = lax.dot_general(xn[...], wv[pl.ds(o, tile), :], (((1,), (1,)), ((), ())), preferred_element_type=F32)
        return 0

    lax.fori_loop(0, full, vocab_tile, 0)
    if full * tile < vocab:
        logits[:, full * tile:] = lax.dot_general(xn[...], wv[full * tile:, :], (((1,), (1,)), ((), ())), preferred_element_type=F32)
    out = pltpu.make_async_copy(logits, logits_h, ld.at[11])
    out.start()

    def drain(c, _):
        for d in range(1, tp):
            ar1_copy(c, me, d, lax.rem(me + d, tp)).wait_send()
            rs2_copy(c, me, d, lax.rem(me + d, tp)).wait_send()

        @pl.when(st < last)
        def _():
            for d in range(tp):
                ag_copy(c, me, d, lax.rem(me + d, tp), st + 1).wait_send()

        @pl.when(st == last)
        def _():
            view = fin.at[pl.ds(0, total - 1)]
            pltpu.make_async_copy(view, view, fin_s.at[c]).wait()

        ks = pl.ds(pl.multiple_of(c * krows, krows), krows)
        pltpu.make_async_copy(kc.at[ks], ko_h.at[ks], lo.at[0, c]).wait()
        pltpu.make_async_copy(vc.at[ks], vo_h.at[ks], lo.at[1, c]).wait()
        return 0

    lax.fori_loop(0, chunks, drain, 0)
    out.wait()


def solution(mesh):
    tp, stages = mesh.shape["tp"], mesh.shape["stage"]
    cache_spec = P('stage', 'replica', None, None, 'tp', None)
    in_specs = (P('replica'), P('stage', None, 'tp', None, None), P('stage', 'tp', None), P('stage', None, 'tp'), P('stage', None, 'tp'), P('stage', 'tp', None), P('stage'), cache_spec, cache_spec, P('replica'), P(), P(None, ('stage', 'tp')))
    out_specs = (P('replica', None, ('stage', 'tp')), cache_spec, cache_spec)

    def device_step(embeds, w_qkv, w_out, w_gate, w_up, w_down, norm_gain, k_cache, v_cache, lengths, final_gain, w_unembed):
        groups, batch, width = embeds.shape
        tokens = groups * batch
        chunks = tokens // ROWS
        cw = width // tp
        _, _, kvs, slots, hd = w_qkv.shape
        ctx = k_cache.shape[3]
        ff = w_gate.shape[2]
        vocab = w_unembed.shape[1]
        crow = tokens * ctx * kvs
        emb = embeds.reshape(chunks, ROWS, tp, cw).transpose(0, 2, 1, 3)
        args = (emb, w_qkv.reshape(width * kvs * slots, hd), w_out[0], w_gate[0], w_up[0], w_down[0], norm_gain[0],
                k_cache.reshape(crow, hd), v_cache.reshape(crow, hd), lengths.T, jnp.asarray(rope_rows(ctx, hd)), final_gain.reshape(1, width), w_unembed.T)
        hbm = pl.BlockSpec(memory_space=pl.ANY)
        in_s = [hbm] * len(args)
        in_s[9] = pl.BlockSpec(memory_space=pltpu.SMEM)
        V = pltpu.VMEM
        dma = pltpu.SemaphoreType.DMA
        qtot = width * kvs * slots
        scratch = [V((qtot, hd), BF16), V((qtot // 8, hd), F32), V((width, kvs * slots * hd), BF16), V(w_out.shape[1:], BF16), V(w_gate.shape[1:], BF16), V(w_up.shape[1:], BF16), V(w_down.shape[1:], BF16),
                   V((2, width), F32), V((crow, hd), BF16), V((crow, hd), BF16), V((2, ctx, hd), F32), V((1, width), F32), V((vocab, width), BF16),
                   V((chunks, tp, ROWS, cw), BF16), V((chunks, tp, ROWS, cw), F32), V((ROWS, ff), F32), V((chunks, tp, ROWS, width), F32), V((chunks, tp, ROWS, cw), F32), V((chunks, tp, ROWS, cw), F32),
                   V((chunks, ROWS, cw), BF16), V((chunks * tp, ROWS, cw), BF16), V((chunks, ROWS, hd), F32), V((chunks, ROWS, hd), F32), V((tokens, width), BF16), V((tokens, vocab), F32),
                   dma((12,)), dma((8,)), dma((2, chunks)), dma((chunks, tp)), dma((chunks, tp)), dma((chunks, tp)), dma((chunks, tp)), dma((chunks, tp)), dma((chunks, tp)), dma((chunks,)), dma((chunks, tp))]
        logits, k_out, v_out = pl.pallas_call(
            functools.partial(step_kernel, (tp, stages, chunks, kvs, slots, hd, ctx)),
            out_shape=[jax.ShapeDtypeStruct((tokens, vocab), F32), jax.ShapeDtypeStruct((crow, hd), BF16), jax.ShapeDtypeStruct((crow, hd), BF16)],
            in_specs=in_s, out_specs=[hbm] * 3, scratch_shapes=scratch, name="decode_step",
            compiler_params=pltpu.CompilerParams(collective_id=0, has_side_effects=True, vmem_limit_bytes=67043328))(*args)
        return logits.reshape(groups, batch, vocab), k_out.reshape(k_cache.shape), v_out.reshape(v_cache.shape)

    return jax.shard_map(device_step, mesh=mesh, in_specs=in_specs, out_specs=out_specs, check_vma=False)
```

time: 2130 us -> 204 us (0.10)
  blocking collectives: 880 us -> 0 us
  matrix products: 574 us -> 0 us
  starting transfers between devices: 431 us -> 0 us
  Pallas kernels: 0 us -> 194 us
  other arithmetic: 149 us -> 0 us
  waiting for transfers between devices: 48.5 us -> 0 us
    psum x78 -> x0, blocking collectives: 880 us -> none  [the longest x39 457 us: stage_layers(): lax.psum(jnp.dot(attn_flat, w_out[layer_idx], preferred_element_type=jnp....]
    dot_general x274 -> x0, matrix products: 574 us -> none  [the longest x39 249 us: stage_layers(): jnp.dot(hidden, w_down[layer_idx], preferred_element_type=jnp.float32)]
    ppermute x39 -> x0, starting transfers between devices: 431 us -> none  [tick_body(): incoming = lax.ppermute(hidden_out, 'stage', next_stage)]
    pallas_call x0 -> x1, Pallas kernels: none -> 194 us  [device_step(): pl.pallas_call(functools.partial(step_kernel, (tp, stages, chunks, kvs, s...]
    dynamic_update_slice x78 -> x0, other arithmetic: 50.3 us -> none  [store_group(): lax.dynamic_update_index_in_dim(store_buf, jnp.where(is_valid, new_rows,...]
    psum x1 -> x0, waiting for transfers between devices: 48.4 us -> none  [device_step(): lax.psum(jnp.where(stage_idx == stages - 1, loop_out[3], jnp.zeros_like(l...]
    reduce_sum x118 -> x0, other arithmetic: 45.1 us -> none  [the longest x79 38.7 us: rms_norm(): mean_sq = jnp.mean(values * values, axis=-1, keepdims=True)]
    convert_element_type x39 -> x0, other arithmetic: 27.8 us -> none  [rope_tables(): angles = lengths.astype(jnp.float32)[..., None] * inv_freq]
  transfers between devices with their start and end apart: 40 -> 0, of which waited for: 1 -> 0; matrix products, arithmetic and copies ran while one was open for 3% -> 0% of each run, Pallas kernels for 0% -> 0%
where the time goes in v1:
time: 204 us
  Pallas kernels  194 us (95%)
  local copies, waits for them, and re-layouts  9.36 us (5%)
    pallas_call x1, Pallas kernels, device_step(): pl.pallas_call(functools.partial(step_kernel, (tp, stages, chunks, kvs, s...  194 us
    unnamed x2, local copies, waits for them, and re-layouts  4.55 us

profile of v1, /device:TPU:97, one launch (start us, length us, event | category | flops | bytes accessed | tf_op | source)
XLA Modules:
  0.0 204.0 jit_solution(15683649960805451004)
XLA Ops:
  0.6 1.1 reshape.30
  1.8 0.8 copy.18
  2.5 194.0 %decode_step.1 = (f32[64,4748]{1,0:T(8,128)}, bf16[2048,128]{1,0:T(8,128)(2,1)}, bf16[2048,128]{1,0:T(8,128)(2,1)}) custom-call(bf16[8,4,8,512]{3,2,1,0:T(8,128)(2,1)} %bitcast.22, bf16[16384,128]{1,0:T(8,128)(2,1)} %bitcast.20, bf16[512,2048]{1,0:T(8,128)(2,1)} %bitcast.21, bf16[2048,1536]{1,0:T(8,128)(2,1)} %bitcast.17, bf16[2048,1536]{1,0:T(8,128)(2,1)} %bitcast.18, ...), custom_call_target="tpu_custom_call" | custom-call | tf_op jit(solution)/shard_map/decode_step/pallas_call | solution.py:364
  196.5 2.9 %reshape.35 = f32[32,2,4748]{2,1,0:T(2,128)} reshape(f32[64,4748]{1,0:T(8,128)} %get-tuple-element.6) | data formatting | bytes 2430976 | tf_op jit(solution)/shard_map/reshape | solution.py:369
  199.4 2.3 %copy.21 = bf16[1,32,2,16,2,128]{5,4,3,2,1,0:T(2,128)(2,1)} copy(bf16[1,32,2,16,2,128]{5,4,3,2,1,0:T(2,128)(2,1)} %bitcast.26) | data formatting | bytes 1048576
  201.7 2.3 %copy.22 = bf16[1,32,2,16,2,128]{5,4,3,2,1,0:T(2,128)(2,1)} copy(bf16[1,32,2,16,2,128]{5,4,3,2,1,0:T(2,128)(2,1)} %bitcast.25) | data formatting | bytes 1048576
